TPU v7x, 32 devices: a whole 2x2x4 slice. The times are simulated.
32 devices in a mesh: mode: 4 (over y, x), mesh: 8 (over z, core).
Axes of the slice: x: 2, y: 2, z: 4, core: 2. Of those that a mesh axis runs over, the one named last changes fastest.
Arguments:
- velocity: float32 [3, 2, 64, 20480], P(None, None, 'mode', 'mesh'), may hold values from -2.1 to 2.1
- magnetic: float32 [3, 2, 64, 20480], P(None, None, 'mode', 'mesh'), may hold values from -2.1 to 2.1
- leaf_inverse: bfloat16 [64, 160, 128, 128], P('mode', 'mesh'), may hold values from -1 to 2
- leaf_coupling: bfloat16 [64, 128, 20480], P('mode', None, 'mesh'), may hold values from -0.05908203 to 0.05908203
- separator_inverse: bfloat16 [64, 1024, 128], P('mode', 'mesh'), may hold values from -1 to 2
- separator_coupling: bfloat16 [64, 1024, 128], P('mode', 'mesh'), may hold values from -0.26367188 to 0.26367188
- separator_source: float32 [2, 64, 1024], P(None, 'mode', 'mesh'), may hold values from -6 to 6
- front_rows: int32 [8, 2, 128], P('mesh'), may hold values from 0 to 127, each once within a row
Outputs:
- nonlinear: float32 [3, 2, 64, 20480], P(None, None, 'mode', 'mesh')
- azimuthal_field: float32 [2, 64, 20480], P(None, 'mode', 'mesh')
- separator_solution: float32 [2, 64, 1024], P(None, 'mode', 'mesh')
Inputs may be any that keep to these rules, and one draw needn't show every extreme that they name: front_rows[p, 0] and front_rows[p, 1] each hold every number below 128 once.
All inputs are finite; a program needn't handle non-finite values.
Results may differ from a plain program's by a relative error of at most 0.015.
Values may be sent and summed in bfloat16 or wider, within the bound.
No kernel may reach another device: no remote copies, remote signals or barrier semaphores. Data moves between devices by JAX's collectives and lax.ppermute only.
A program may use at most 128 MiB of HBM per device.

v0:
```python
import jax
import jax.numpy as jnp
from jax import lax
from jax.sharding import PartitionSpec as P

M = 64
NPHI = 192
highest = lax.Precision.HIGHEST
dt_step = 0.5


def tables():
    angles = jnp.arange(NPHI, dtype=jnp.int32)[:, None]
    orders = jnp.arange(M, dtype=jnp.int32)[None, :]
    phase = (angles * orders % NPHI).astype(jnp.float32) * (2.0 * jnp.pi / NPHI)
    forward = jnp.stack([jnp.cos(phase), jnp.sin(phase)], axis=1)
    weights = jnp.where(orders == 0, 1.0, 2.0).astype(jnp.float32) / NPHI
    backward = jnp.stack([(jnp.cos(phase) * weights).T, (jnp.sin(phase) * weights).T], axis=0)
    return (forward, backward)


def cross_terms(first, second):
    return jnp.stack(
        [
            first[1] * second[2] - first[2] * second[1],
            first[2] * second[0] - first[0] * second[2],
            first[0] * second[1] - first[1] * second[0],
        ]
    )


def forward_fields(forward, velocity, magnetic):
    return (
        jnp.einsum("kam,camn->ckn", forward, velocity, precision=highest),
        jnp.einsum("kam,camn->ckn", forward, magnetic, precision=highest),
    )


def gather_children(values):
    return lax.all_gather(values, "mesh", axis=2, tiled=True)


def gather_parents(values):
    return lax.all_gather(values, "mesh", axis=2, tiled=True)


def block_of(whole, index, partitions, sep_rows):
    start = (jnp.clip(index, 0, partitions - 1) * sep_rows).astype(jnp.int32)
    return lax.dynamic_slice_in_dim(whole, start, sep_rows, 2)


def shards(
    velocity,
    magnetic,
    leaf_inverse,
    leaf_coupling,
    separator_inverse,
    separator_coupling,
    separator_source,
    front_rows,
):
    modes_dev = velocity.shape[2]
    nodes_dev = velocity.shape[3]
    forward, backward = tables()
    spread_velocity, spread_magnetic = (
        lax.all_to_all(
            velocity.astype(jnp.bfloat16), "mode", split_axis=3, concat_axis=2, tiled=True
        ).astype(velocity.dtype),
        lax.all_to_all(
            magnetic.astype(jnp.bfloat16), "mode", split_axis=3, concat_axis=2, tiled=True
        ).astype(magnetic.dtype),
    )
    phys_velocity, phys_magnetic = forward_fields(forward, spread_velocity, spread_magnetic)
    local_terms = jnp.einsum(
        "amk,ckn->camn", backward, cross_terms(phys_velocity, phys_magnetic), precision=highest
    )
    nonlinear = lax.all_to_all(
        local_terms.astype(jnp.bfloat16), "mode", split_axis=2, concat_axis=3, tiled=True
    ).astype(local_terms.dtype)
    blocks_dev = leaf_inverse.shape[1]
    block_width = leaf_inverse.shape[2]
    sep_rows = separator_source.shape[2]
    source = (magnetic[1] + dt_step * nonlinear[1]).astype(jnp.bfloat16)
    leaf_solved = (
        jnp.einsum(
            "mkij,cmkj->cmki",
            leaf_inverse,
            source.reshape(2, modes_dev, blocks_dev, block_width),
            preferred_element_type=jnp.float32,
        )
        .reshape(2, modes_dev, nodes_dev)
        .astype(jnp.bfloat16)
    )
    row_order = front_rows[0]
    leaf_map = jnp.take(leaf_coupling, row_order[0], axis=1)
    upward_map = jnp.take(separator_coupling, row_order[1], axis=1)
    leaf_update = jnp.einsum(
        "mij,cmj->cmi", leaf_map, leaf_solved, preferred_element_type=jnp.float32
    )
    partitions = lax.axis_size("mesh")
    levels = partitions.bit_length() - 1
    position = lax.axis_index("mesh")
    depth_now = sum(
        [(position % 2**bit_now == 0).astype(jnp.int32) for bit_now in range(1, levels + 1)]
    )
    level_here = depth_now + 1

    def settle(arrived, height, reduced, outgoing):
        fresh = jnp.einsum(
            "mij,cmj->cmi",
            separator_inverse,
            (separator_source - arrived).astype(jnp.bfloat16),
            preferred_element_type=jnp.float32,
        ).astype(jnp.bfloat16)
        sending = jnp.einsum("mij,cmj->cmi", upward_map, fresh, preferred_element_type=jnp.float32)
        active = level_here == height
        return (jnp.where(active, fresh, reduced), jnp.where(active, sending, outgoing))

    reduced = jnp.zeros(separator_source.shape, jnp.bfloat16)
    outgoing = jnp.zeros(separator_source.shape, jnp.float32)
    everyone = gather_children(leaf_update)
    arrived = block_of(everyone, position - 1, partitions, sep_rows) + block_of(
        everyone, position, partitions, sep_rows
    )
    reduced, outgoing = settle(arrived, 1, reduced, outgoing)
    for height in range(2, levels + 1):
        gap = 2 ** (height - 2)
        everyone = gather_children(outgoing)
        arrived = block_of(everyone, position - gap, partitions, sep_rows) + block_of(
            everyone, position + gap, partitions, sep_rows
        )
        reduced, outgoing = settle(arrived, height, reduced, outgoing)
    everyone = gather_children(outgoing)
    reduced, outgoing = settle(
        block_of(everyone, partitions // 2, partitions, sep_rows), levels + 1, reduced, outgoing
    )
    top_value = jnp.einsum(
        "mij,cmi->cmj", separator_inverse, reduced, preferred_element_type=jnp.float32
    )
    solution = jnp.where(
        level_here == levels + 1, top_value, jnp.zeros(separator_source.shape, jnp.float32)
    )
    for height in range(levels, 0, -1):
        everyone = gather_parents(solution.astype(jnp.bfloat16))
        if height == levels:
            parent = position * 0
        else:
            parent = position // 2 ** (height + 1) * 2 ** (height + 1) + 2**height
        above = block_of(everyone, parent, partitions, sep_rows)
        residue = reduced.astype(jnp.float32) - jnp.einsum(
            "mij,cmi->cmj", upward_map, above, preferred_element_type=jnp.float32
        )
        fresh = jnp.einsum(
            "mij,cmi->cmj",
            separator_inverse,
            residue.astype(jnp.bfloat16),
            preferred_element_type=jnp.float32,
        )
        solution = jnp.where(level_here == height, fresh, solution)
    everyone = gather_parents(solution.astype(jnp.bfloat16))
    above = block_of(everyone, 2 * (position // 2) + 1, partitions, sep_rows)
    residue = leaf_solved.astype(jnp.float32) - jnp.einsum(
        "mij,cmi->cmj", leaf_map, above, preferred_element_type=jnp.float32
    )
    azimuthal_field = jnp.einsum(
        "mkji,cmkj->cmki",
        leaf_inverse,
        residue.astype(jnp.bfloat16).reshape(2, modes_dev, blocks_dev, block_width),
        preferred_element_type=jnp.float32,
    ).reshape(2, modes_dev, nodes_dev)
    return (nonlinear, azimuthal_field, solution)


def solution(mesh):
    in_specs = (
        P(None, None, "mode", "mesh"),
        P(None, None, "mode", "mesh"),
        P("mode", "mesh", None, None),
        P("mode", None, "mesh"),
        P("mode", "mesh", None),
        P("mode", "mesh", None),
        P(None, "mode", "mesh"),
        P("mesh", None, None),
    )
    out_specs = (P(None, None, "mode", "mesh"), P(None, "mode", "mesh"), P(None, "mode", "mesh"))
    return jax.shard_map(shards, mesh=mesh, in_specs=in_specs, out_specs=out_specs, check_vma=False)
```

profile of v0, /device:TPU:0, one launch (start us, length us, event | category | flops | bytes accessed | tf_op | source)
XLA Modules:
  0.0 205.2 jit_solution(15129035748217924793)
XLA Ops:
  0.7 1.4 convert_element_type.163
  2.0 5.2 %copy.84 = bf16[3,2,16,2560]{2,0,1,3:T(4,128)(2,1)} copy(bf16[3,2,16,2560]{3,2,1,0:T(8,128)(2,1)S(1)} %convert_element_type.163) | data formatting | bytes 983040 | tf_op jit(solution)/shard_map/convert_element_type | solution.py:70
  7.2 6.7 %reshape.281 = bf16[4,2,30720]{2,1,0:T(2,128)(2,1)} reshape(bf16[2560,2,3,16]{3,2,1,0:T(4,128)(2,1)} %bitcast.190) | data formatting | bytes 983040
  13.9 5.2 %all-to-all-start.1 = ((bf16[4,2,30720]{2,1,0:T(2,128)(2,1)}), bf16[4,2,30720]{2,1,0:T(2,128)(2,1)S(1)}, u32[]{:S(2)}, u32[]{:S(2)}) async-start(bf16[4,2,30720]{2,1,0:T(2,128)(2,1)} %reshape.281), calls=%async_computation.1 | async-start | bytes 983040 | tf_op jit(solution)/shard_map/all_to_all | solution.py:69
  19.1 5.2 %copy.82 = bf16[3,2,16,2560]{2,0,1,3:T(4,128)(2,1)} copy(bf16[3,2,16,2560]{3,2,1,0:T(8,128)(2,1)S(1)} %convert_element_type.162) | data formatting | bytes 983040 | tf_op jit(solution)/shard_map/convert_element_type | solution.py:67
  24.3 6.7 %reshape.279 = bf16[4,2,30720]{2,1,0:T(2,128)(2,1)} reshape(bf16[2560,2,3,16]{3,2,1,0:T(4,128)(2,1)} %bitcast.191) | data formatting | bytes 983040
  31.0 4.2 %all-to-all-start = ((bf16[4,2,30720]{2,1,0:T(2,128)(2,1)}), bf16[4,2,30720]{2,1,0:T(2,128)(2,1)S(1)}, u32[]{:S(2)}, u32[]{:S(2)}) async-start(bf16[4,2,30720]{2,1,0:T(2,128)(2,1)} %reshape.279), calls=%async_computation | async-start | bytes 983040 | tf_op jit(solution)/shard_map/all_to_all | solution.py:66
  35.2 0.3 fusion.66
  35.5 0.3 cosine_multiply_fusion
  35.8 6.0 %reshape.282 = bf16[2560,2,3,16]{3,2,1,0:T(4,128)(2,1)} reshape(bf16[4,2,30720]{2,1,0:T(2,128)(2,1)S(1)} %all-to-all-done.1) | data formatting | bytes 983040
  41.8 5.8 %copy.85 = bf16[3,2,16,4,640]{4,2,3,1,0:T(8,128)(2,1)S(1)} copy(bf16[3,2,16,4,640]{2,0,1,4,3:T(4,128)(2,1)} %bitcast.192) | data formatting | bytes 983040 | tf_op jit(solution)/shard_map/all_to_all | solution.py:69
  47.5 6.0 %reshape.280 = bf16[2560,2,3,16]{3,2,1,0:T(4,128)(2,1)} reshape(bf16[4,2,30720]{2,1,0:T(2,128)(2,1)S(1)} %all-to-all-done) | data formatting | bytes 983040
  53.5 5.8 %copy.83 = bf16[3,2,16,4,640]{4,2,3,1,0:T(8,128)(2,1)S(1)} copy(bf16[3,2,16,4,640]{2,0,1,4,3:T(4,128)(2,1)} %bitcast.193) | data formatting | bytes 983040 | tf_op jit(solution)/shard_map/all_to_all | solution.py:66
  59.3 0.8 convolution_bitcast_fusion
  60.1 0.8 convolution_bitcast_fusion.1
  60.9 0.2 multiply_subtract_fusion.2
  61.1 1.2 fusion.19
  62.3 1.3 copy.86
  63.5 4.2 %all-to-all-start.2 = ((bf16[3,2,64,640]{3,1,0,2:T(2,128)(2,1)}), bf16[3,2,64,640]{3,1,0,2:T(2,128)(2,1)S(1)}, u32[]{:S(2)}, u32[]{:S(2)}) async-start(bf16[3,2,64,640]{3,1,0,2:T(2,128)(2,1)} %copy.86), calls=%async_computation.2 | async-start | bytes 983040 | tf_op jit(solution)/shard_map/all_to_all | solution.py:77
  67.9 2.8 %gather_fusion.1 = bf16[128,16,128]{2,0,1:T(8,128)(2,1)S(1)} fusion(bf16[16,128,128]{2,1,0:T(8,128)(2,1)S(1)} %copy-done, s32[1024]{0:T(1024)S(1)} %pad_clamp_fusion), kind=kCustom, calls=%fused_computation.1 | custom fusion | bytes 1049088 | tf_op jit(solution)/shard_map/jit(_take)/gather | solution.py:96
  70.6 24.7 %gather_fusion = bf16[128,16,2560]{2,0,1:T(8,128)(2,1)} fusion(bf16[16,128,2560]{2,1,0:T(8,128)(2,1)} %param.11, s32[1024]{0:T(1024)S(1)} %pad_clamp_fusion.1), kind=kCustom, calls=%fused_computation | custom fusion | bytes 20972032 | tf_op jit(solution)/shard_map/jit(_take)/gather | solution.py:95
  95.5 1.0 add_convert_fusion
  96.5 0.1 convert_element_type.172
  96.6 1.0 copy.104
  97.6 9.0 %fusion.20 = bf16[2,16,2560]{2,0,1:T(2,128)(2,1)S(1)} fusion(bf16[16,20,128,128]{3,2,1,0:T(8,128)(2,1)} %param.10, bf16[2,16,20,128]{3,2,1,0:T(8,128)(2,1)S(1)} %convert_element_type.172), kind=kOutput, calls=%fused_computation.22 | convolution fusion | flops 21053440 | bytes 10813440 | tf_op jit(solution)/shard_map/mkij,cmkj->cmki/dot_general | solution.py:85
  106.7 2.9 %fusion.26 = f32[2,16,128]{2,0,1:T(2,128)S(1)} fusion(bf16[2,16,2560]{2,0,1:T(2,128)(2,1)S(1)} %fusion.20, bf16[128,16,2560]{2,0,1:T(8,128)(2,1)S(1)} %copy-done.2, pred[128]{0:T(512)(128)(4,1)S(1)} %get-tuple-element.25), kind=kOutput, calls=%fused_computation.24 | convolution fusion | flops 26214400 | bytes 10666112 | tf_op jit(solution)/shard_map/mij,cmj->cmi/dot_general | solution.py:97
  109.5 12.5 %all_gather.24 = f32[2,16,1024]{2,0,1:T(2,128)S(1)} all-gather(f32[2,16,128]{2,0,1:T(2,128)S(1)} %fusion.26), channel_id=1, replica_groups=mesh['mode'=4,'mesh'=8] {'mesh'}, dimensions={2}, use_global_device_ids=true | all-gather | bytes 147456 | tf_op jit(solution)/shard_map/all_gather | solution.py:40
  122.1 0.4 fusion.39
  122.4 0.4 fusion.35
  122.9 9.3 %all_gather.25 = f32[2,16,1024]{2,0,1:T(2,128)S(1)} all-gather(f32[2,16,128]{2,0,1:T(2,128)S(1)} %fusion.35), channel_id=1, replica_groups=mesh['mode'=4,'mesh'=8] {'mesh'}, dimensions={2}, use_global_device_ids=true | all-gather | bytes 147456 | tf_op jit(solution)/shard_map/all_gather | solution.py:40
  132.2 0.4 fusion.40
  132.5 0.4 fusion.34
  133.0 10.6 %all_gather.26 = f32[2,16,1024]{2,0,1:T(2,128)S(1)} all-gather(f32[2,16,128]{2,0,1:T(2,128)S(1)} %fusion.34), channel_id=1, replica_groups=mesh['mode'=4,'mesh'=8] {'mesh'}, dimensions={2}, use_global_device_ids=true | all-gather | bytes 147456 | tf_op jit(solution)/shard_map/all_gather | solution.py:40
  143.6 0.4 fusion.41
  143.9 0.4 fusion.33
  144.4 9.3 %all_gather.27 = f32[2,16,1024]{2,0,1:T(2,128)S(1)} all-gather(f32[2,16,128]{2,0,1:T(2,128)S(1)} %fusion.33), channel_id=1, replica_groups=mesh['mode'=4,'mesh'=8] {'mesh'}, dimensions={2}, use_global_device_ids=true | all-gather | bytes 147456 | tf_op jit(solution)/shard_map/all_gather | solution.py:40
  153.7 0.4 fusion.43
  154.0 0.3 convolution_select_fusion.3
  154.3 10.3 %all_gather.28 = bf16[2,16,1024]{2,0,1:T(2,128)(2,1)S(1)} all-gather(bf16[2,16,128]{2,0,1:T(2,128)(2,1)S(1)} %convert_bitcast_fusion.2), channel_id=1, replica_groups=mesh['mode'=4,'mesh'=8] {'mesh'}, dimensions={2}, use_global_device_ids=true | all-gather | bytes 73728 | tf_op jit(solution)/shard_map/all_gather | solution.py:44
  164.6 0.4 convolution_select_fusion.2
  165.1 9.0 %all_gather.29 = bf16[2,16,1024]{2,0,1:T(2,128)(2,1)S(1)} all-gather(bf16[2,16,128]{2,0,1:T(2,128)(2,1)S(1)} %convert_bitcast_fusion.1), channel_id=1, replica_groups=mesh['mode'=4,'mesh'=8] {'mesh'}, dimensions={2}, use_global_device_ids=true | all-gather | bytes 73728 | tf_op jit(solution)/shard_map/all_gather | solution.py:44
  174.1 0.4 convolution_select_fusion.1
  174.6 10.3 %all_gather.30 = bf16[2,16,1024]{2,0,1:T(2,128)(2,1)S(1)} all-gather(bf16[2,16,128]{2,0,1:T(2,128)(2,1)S(1)} %convert_bitcast_fusion), channel_id=1, replica_groups=mesh['mode'=4,'mesh'=8] {'mesh'}, dimensions={2}, use_global_device_ids=true | all-gather | bytes 73728 | tf_op jit(solution)/shard_map/all_gather | solution.py:44
  184.9 0.4 fusion.105
  185.3 0.6 copy.98
  186.0 9.1 %all_gather.31 = bf16[2,16,1024]{2,0,1:T(2,128)(2,1)S(1)} all-gather(bf16[2,16,128]{2,0,1:T(2,128)(2,1)S(1)} %get-tuple-element.30), channel_id=1, replica_groups=mesh['mode'=4,'mesh'=8] {'mesh'}, dimensions={2}, use_global_device_ids=true | all-gather | bytes 73728 | tf_op jit(solution)/shard_map/all_gather | solution.py:44
  195.1 9.3 %convolution_bitcast_fusion.2 = f32[2,16,20,128]{3,0,2,1:T(2,128)S(1)} fusion(bf16[16,20,128,128]{3,2,1,0:T(8,128)(2,1)} %param.10, bf16[128,16,2560]{2,0,1:T(8,128)(2,1)} %gather_fusion, pred[128]{0:T(512)(128)(4,1)S(1)} %get-tuple-element.25, bf16[2,16,2560]{2,0,1:T(2,128)(2,1)S(1)} %fusion.20, bf16[2,16,1024]{2,0,1:T(2,128)(2,1)S(1)} %all_gather.31, ...), kind=kOutput, calls=%fused_computation.20 | convolution fusion | flops 47431680 | bytes 21471748 | tf_op jit(solution)/shard_map/mkji,cmkj->cmki/dot_general | solution.py:165
  204.5 0.8 reshape.255
  (30 shorter events, 0.3 us)
Async XLA Ops:
  0.6 67.2 %copy-start = (bf16[16,128,128]{2,1,0:T(8,128)(2,1)S(1)}, bf16[16,128,128]{2,1,0:T(8,128)(2,1)}, u32[]{:S(2)}) copy-start(bf16[16,128,128]{2,1,0:T(8,128)(2,1)} %param.13) | copy-start | bytes 1572868
  0.6 18.4 %copy-start.4 = (f32[3,2,16,2560]{3,2,1,0:T(8,128)S(1)}, f32[3,2,16,2560]{3,2,1,0:T(8,128)}, u32[]{:S(2)}) copy-start(f32[3,2,16,2560]{3,2,1,0:T(8,128)} %param.8) | copy-start | bytes 2949124
  7.2 23.8 %copy-start.6 = (s32[1,2,128]{2,1,0:T(2,128)S(1)}, s32[1,2,128]{2,1,0:T(2,128)}, u32[]{:S(2)}) copy-start(s32[1,2,128]{2,1,0:T(2,128)} %param.15) | copy-start | bytes 3076
  13.9 17.1 %all-to-all-start.1 = ((bf16[4,2,30720]{2,1,0:T(2,128)(2,1)}), bf16[4,2,30720]{2,1,0:T(2,128)(2,1)S(1)}, u32[]{:S(2)}, u32[]{:S(2)}) async-start(bf16[4,2,30720]{2,1,0:T(2,128)(2,1)} %reshape.281), calls=%async_computation.1 | async-start | bytes 983040 | tf_op jit(solution)/shard_map/all_to_all | solution.py:69
  31.0 16.5 %all-to-all-start = ((bf16[4,2,30720]{2,1,0:T(2,128)(2,1)}), bf16[4,2,30720]{2,1,0:T(2,128)(2,1)S(1)}, u32[]{:S(2)}, u32[]{:S(2)}) async-start(bf16[4,2,30720]{2,1,0:T(2,128)(2,1)} %reshape.279), calls=%async_computation | async-start | bytes 983040 | tf_op jit(solution)/shard_map/all_to_all | solution.py:66
  63.5 31.8 %all-to-all-start.2 = ((bf16[3,2,64,640]{3,1,0,2:T(2,128)(2,1)}), bf16[3,2,64,640]{3,1,0,2:T(2,128)(2,1)S(1)}, u32[]{:S(2)}, u32[]{:S(2)}) async-start(bf16[3,2,64,640]{3,1,0,2:T(2,128)(2,1)} %copy.86), calls=%async_computation.2 | async-start | bytes 983040 | tf_op jit(solution)/shard_map/all_to_all | solution.py:77
  96.6 10.1 %copy-start.2 = (bf16[128,16,2560]{2,0,1:T(8,128)(2,1)S(1)}, bf16[128,16,2560]{2,0,1:T(8,128)(2,1)}, u32[]{:S(2)}) copy-start(bf16[128,16,2560]{2,0,1:T(8,128)(2,1)} %gather_fusion) | copy-start | bytes 31457284
  106.6 15.4 %copy-start.3 = (bf16[16,128,128]{2,1,0:T(8,128)(2,1)S(1)}, bf16[16,128,128]{2,1,0:T(8,128)(2,1)}, u32[]{:S(2)}) copy-start(bf16[16,128,128]{2,1,0:T(8,128)(2,1)} %param.12) | copy-start | bytes 1572868
  106.6 15.4 %copy-start.5 = (f32[2,16,128]{2,1,0:T(8,128)S(1)}, f32[2,16,128]{2,1,0:T(8,128)}, u32[]{:S(2)}) copy-start(f32[2,16,128]{2,1,0:T(8,128)} %param.14) | copy-start | bytes 49156
  186.0 19.3 %copy-start.1 = (bf16[16,128,128]{2,1,0:T(8,128)(2,1)S(1)}, bf16[16,128,128]{2,1,0:T(8,128)(2,1)}, u32[]{:S(2)}) copy-start(bf16[16,128,128]{2,1,0:T(8,128)(2,1)} %param.13) | copy-start | bytes 1572868
where the time goes:
time: 206 us; the launch traced here: 205 us
  blocking collectives  80.5 us (39%)
  local copies, waits for them, and re-layouts  78.6 us (38%)
  matrix products  28.4 us (14%)
  starting transfers between devices  13.6 us (7%)
  other arithmetic  3.23 us (2%)
    all_gather x4, blocking collectives, gather_children(): return lax.all_gather(values, 'mesh', axis=2, tiled=True)  41.7 us
    all_gather x4, blocking collectives, gather_parents(): return lax.all_gather(values, 'mesh', axis=2, tiled=True)  38.7 us
    unnamed x19, local copies, waits for them, and re-layouts  25.9 us
    gather x1, local copies, waits for them, and re-layouts, shards(): leaf_map = jnp.take(leaf_coupling, row_order[0], axis=1)  24.7 us
    dot_general x1, matrix products, shards(): jnp.einsum('mkji,cmkj->cmki', leaf_inverse, residue.astype(jnp.bfloat16)....  9.34 us
    dot_general x1, matrix products, shards(): jnp.einsum('mkij,cmkj->cmki', leaf_inverse, source.reshape(2, modes_dev,...  8.98 us
    all_to_all x1, local copies, waits for them, and re-layouts, shards(): lax.all_to_all(magnetic.astype(jnp.bfloat16), 'mode', split_axis=3, conca...  5.77 us
    all_to_all x1, local copies, waits for them, and re-layouts, shards(): lax.all_to_all(velocity.astype(jnp.bfloat16), 'mode', split_axis=3, conca...  5.77 us
  transfers between devices with their start and end apart: 3, of which 0 were waited for; matrix products, arithmetic and copies ran while one was open for 25% of the time, Pallas kernels for 0%

commit v1 on v0

--- a/solution.py
+++ b/solution.py
@@ -7,6 +7,29 @@
 NPHI = 192
 highest = lax.Precision.HIGHEST
 dt_step = 0.5
+
+
+def cut_along(array, dim, size):
+    lengths = array.shape
+    pieces = array.reshape(*lengths[:dim], size, lengths[dim] // size, *lengths[dim + 1 :])
+    return jnp.moveaxis(pieces, dim, 0)
+
+
+def in_order(parts, dim):
+    parts = jnp.moveaxis(parts, 0, dim)
+    shape = parts.shape
+    return parts.reshape(*shape[:dim], shape[dim] * shape[dim + 1], *shape[dim + 2 :])
+
+
+def swapped_with_each(shard, axis, split_dim, concat_dim):
+    size, here = (lax.axis_size(axis), lax.axis_index(axis))
+    blocks = cut_along(shard, split_dim, size)
+    outs = [blocks[here]]
+    for lap in range(1, size):
+        sent = blocks[here ^ lap]
+        outs.append(lax.ppermute(sent, axis, [(i, i ^ lap) for i in range(size)]))
+    blocks = jnp.stack(outs)[here ^ jnp.arange(size)]
+    return in_order(blocks, concat_dim)
 
 
 def tables():
@@ -66,9 +89,7 @@
         lax.all_to_all(
             velocity.astype(jnp.bfloat16), "mode", split_axis=3, concat_axis=2, tiled=True
         ).astype(velocity.dtype),
-        lax.all_to_all(
-            magnetic.astype(jnp.bfloat16), "mode", split_axis=3, concat_axis=2, tiled=True
-        ).astype(magnetic.dtype),
+        swapped_with_each(magnetic.astype(jnp.bfloat16), "mode", 3, 2).astype(magnetic.dtype),
     )
     phys_velocity, phys_magnetic = forward_fields(forward, spread_velocity, spread_magnetic)
     local_terms = jnp.einsum(

time: 206 us -> 189 us (0.917)
  local copies, waits for them, and re-layouts: 78.6 us -> 56.9 us
  waiting for transfers between devices: 0.01 us -> 4.57 us
    unnamed x19 -> x17, local copies, waits for them, and re-layouts: 25.9 us -> 13.3 us
    all_to_all x1 -> x0, local copies, waits for them, and re-layouts: 5.77 us -> none  [shards(): lax.all_to_all(magnetic.astype(jnp.bfloat16), 'mode', split_axis=3, conca...]
    all_to_all x1 -> x0, starting transfers between devices: 5.19 us -> none  [shards(): lax.all_to_all(magnetic.astype(jnp.bfloat16), 'mode', split_axis=3, conca...]
    convert_element_type x1 -> x0, local copies, waits for them, and re-layouts: 5.18 us -> none  [shards(): magnetic.astype(jnp.bfloat16)]
    ppermute x0 -> x3, starting transfers between devices: none -> 4.69 us  [swapped_with_each(): outs.append(lax.ppermute(sent, axis, [(i, i ^ lap) for i in range(size)]))]
    all_to_all x1, waiting for transfers between devices: 0.01 us -> 4.56 us  [shards(): lax.all_to_all(velocity.astype(jnp.bfloat16), 'mode', split_axis=3, conca...]
  transfers between devices with their start and end apart: 3 -> 5, of which waited for: 0 -> 1; matrix products, arithmetic and copies ran while one was open for 25% -> 23% of each run, Pallas kernels for 0% -> 0%
where the time goes in v1:
time: 189 us; the launch traced here: 188 us
  blocking collectives  80.3 us (42%)
  local copies, waits for them, and re-layouts  56.9 us (30%)
  matrix products  28.4 us (15%)
  starting transfers between devices  12.3 us (7%)
  waiting for transfers between devices  4.57 us (2%)
  other arithmetic  4.55 us (2%)
    all_gather x4, blocking collectives, gather_children(): return lax.all_gather(values, 'mesh', axis=2, tiled=True)  41.7 us
    all_gather x4, blocking collectives, gather_parents(): return lax.all_gather(values, 'mesh', axis=2, tiled=True)  38.6 us
    gather x1, local copies, waits for them, and re-layouts, shards(): leaf_map = jnp.take(leaf_coupling, row_order[0], axis=1)  24.7 us
    unnamed x17, local copies, waits for them, and re-layouts  13.3 us
    dot_general x1, matrix products, shards(): jnp.einsum('mkji,cmkj->cmki', leaf_inverse, residue.astype(jnp.bfloat16)....  9.34 us
    dot_general x1, matrix products, shards(): jnp.einsum('mkij,cmkj->cmki', leaf_inverse, source.reshape(2, modes_dev,...  8.98 us
    all_to_all x1, local copies, waits for them, and re-layouts, shards(): lax.all_to_all(velocity.astype(jnp.bfloat16), 'mode', split_axis=3, conca...  5.77 us
    convert_element_type x1, local copies, waits for them, and re-layouts, shards(): velocity.astype(jnp.bfloat16)  5.18 us
  transfers between devices with their start and end apart: 5, of which 1 were waited for; matrix products, arithmetic and copies ran while one was open for 23% of the time, Pallas kernels for 0%

profile of v1, /device:TPU:0, one launch (start us, length us, event | category | flops | bytes accessed | tf_op | source)
XLA Modules:
  0.0 188.1 jit_solution(12196699642407343523)
XLA Ops:
  0.7 1.3 convert_element_type.163
  2.1 1.0 constant_dynamic-slice_fusion.3
  3.2 3.0 %collective-permute-start = (bf16[3,2,16,640]{3,2,1,0:T(8,128)(2,1)S(1)}, bf16[3,2,16,640]{3,2,1,0:T(8,128)(2,1)S(1)}, u32[]{:S(2)}, u32[]{:S(2)}) collective-permute-start(bf16[3,2,16,640]{3,2,1,0:T(8,128)(2,1)S(1)} %bitcast.217), channel_id=1, source_target_pairs={{0,8},{8,0},{16,24},{24,16},{1,9},{9,1},{17,25},{25,17},{2,10},{10... | collective-permute-start | bytes 368648 | tf_op jit(solution)/shard_map/ppermute | solution.py:30
  6.2 1.6 collective-permute-start.1
  7.9 1.3 convert_element_type.162
  9.2 5.2 %copy.90 = bf16[3,2,16,2560]{2,0,1,3:T(4,128)(2,1)} copy(bf16[3,2,16,2560]{3,2,1,0:T(8,128)(2,1)S(1)} %convert_element_type.162) | data formatting | bytes 983040 | tf_op jit(solution)/shard_map/convert_element_type | solution.py:90
  14.4 6.7 %reshape.318 = bf16[4,2,30720]{2,1,0:T(2,128)(2,1)} reshape(bf16[2560,2,3,16]{3,2,1,0:T(4,128)(2,1)} %bitcast.205) | data formatting | bytes 983040
  21.0 4.2 %all-to-all-start = ((bf16[4,2,30720]{2,1,0:T(2,128)(2,1)}), bf16[4,2,30720]{2,1,0:T(2,128)(2,1)S(1)}, u32[]{:S(2)}, u32[]{:S(2)}) async-start(bf16[4,2,30720]{2,1,0:T(2,128)(2,1)} %reshape.318), calls=%async_computation | async-start | bytes 983040 | tf_op jit(solution)/shard_map/all_to_all | solution.py:89
  25.2 0.3 fusion.66
  25.5 0.3 cosine_multiply_fusion
  26.0 0.6 gather_fusion
  26.7 0.8 convolution_bitcast_fusion
  27.4 4.6 %all-to-all-done = bf16[4,2,30720]{2,1,0:T(2,128)(2,1)S(1)} async-done(((bf16[4,2,30720]{2,1,0:T(2,128)(2,1)}), bf16[4,2,30720]{2,1,0:T(2,128)(2,1)S(1)}, u32[]{:S(2)}, u32[]{:S(2)}) %all-to-all-start) | async-done | bytes 491552 | tf_op jit(solution)/shard_map/all_to_all | solution.py:89
  32.0 6.0 %reshape.319 = bf16[2560,2,3,16]{3,2,1,0:T(4,128)(2,1)} reshape(bf16[4,2,30720]{2,1,0:T(2,128)(2,1)S(1)} %all-to-all-done) | data formatting | bytes 983040
  38.0 5.8 %copy.91 = bf16[3,2,16,4,640]{4,2,3,1,0:T(8,128)(2,1)S(1)} copy(bf16[3,2,16,4,640]{2,0,1,4,3:T(4,128)(2,1)} %bitcast.206) | data formatting | bytes 983040 | tf_op jit(solution)/shard_map/all_to_all | solution.py:89
  43.7 0.8 convolution_bitcast_fusion.1
  44.5 0.2 multiply_subtract_fusion.2
  44.8 1.2 fusion.19
  46.0 1.3 copy.93
  47.2 3.5 %all-to-all-start.1 = ((bf16[3,2,64,640]{3,1,0,2:T(2,128)(2,1)}), bf16[3,2,64,640]{3,1,0,2:T(2,128)(2,1)S(1)}, u32[]{:S(2)}, u32[]{:S(2)}) async-start(bf16[3,2,64,640]{3,1,0,2:T(2,128)(2,1)} %copy.93), calls=%async_computation.1 | async-start | bytes 983040 | tf_op jit(solution)/shard_map/all_to_all | solution.py:98
  50.9 2.8 %gather_fusion.2 = bf16[128,16,128]{2,0,1:T(8,128)(2,1)S(1)} fusion(bf16[16,128,128]{2,1,0:T(8,128)(2,1)S(1)} %copy-done, s32[1024]{0:T(1024)S(1)} %pad_clamp_fusion), kind=kCustom, calls=%fused_computation.2 | custom fusion | bytes 1049088 | tf_op jit(solution)/shard_map/jit(_take)/gather | solution.py:117
  53.6 24.7 %gather_fusion.1 = bf16[128,16,2560]{2,0,1:T(8,128)(2,1)} fusion(bf16[16,128,2560]{2,1,0:T(8,128)(2,1)} %param.11, s32[1024]{0:T(1024)S(1)} %pad_clamp_fusion.1), kind=kCustom, calls=%fused_computation.1 | custom fusion | bytes 20972032 | tf_op jit(solution)/shard_map/jit(_take)/gather | solution.py:116
  78.4 1.0 add_convert_fusion
  79.6 1.0 copy.115
  80.6 9.0 %fusion.20 = bf16[2,16,2560]{2,0,1:T(2,128)(2,1)S(1)} fusion(bf16[16,20,128,128]{3,2,1,0:T(8,128)(2,1)} %param.10, bf16[2,16,20,128]{3,2,1,0:T(8,128)(2,1)S(1)} %convert_element_type.172), kind=kOutput, calls=%fused_computation.23 | convolution fusion | flops 21053440 | bytes 10813440 | tf_op jit(solution)/shard_map/mkij,cmkj->cmki/dot_general | solution.py:106
  89.7 2.9 %fusion.26 = f32[2,16,128]{2,0,1:T(2,128)S(1)} fusion(bf16[2,16,2560]{2,0,1:T(2,128)(2,1)S(1)} %fusion.20, bf16[128,16,2560]{2,0,1:T(8,128)(2,1)S(1)} %copy-done.1, pred[128]{0:T(512)(128)(4,1)S(1)} %get-tuple-element.32), kind=kOutput, calls=%fused_computation.25 | convolution fusion | flops 26214400 | bytes 10666112 | tf_op jit(solution)/shard_map/mij,cmj->cmi/dot_general | solution.py:118
  92.5 12.5 %all_gather.24 = f32[2,16,1024]{2,0,1:T(2,128)S(1)} all-gather(f32[2,16,128]{2,0,1:T(2,128)S(1)} %fusion.26), channel_id=1, replica_groups=mesh['mode'=4,'mesh'=8] {'mesh'}, dimensions={2}, use_global_device_ids=true | all-gather | bytes 147456 | tf_op jit(solution)/shard_map/all_gather | solution.py:63
  105.1 0.4 fusion.39
  105.4 0.4 fusion.35
  105.9 9.3 %all_gather.25 = f32[2,16,1024]{2,0,1:T(2,128)S(1)} all-gather(f32[2,16,128]{2,0,1:T(2,128)S(1)} %fusion.35), channel_id=1, replica_groups=mesh['mode'=4,'mesh'=8] {'mesh'}, dimensions={2}, use_global_device_ids=true | all-gather | bytes 147456 | tf_op jit(solution)/shard_map/all_gather | solution.py:63
  115.2 0.4 fusion.40
  115.5 0.4 fusion.34
  116.0 10.6 %all_gather.26 = f32[2,16,1024]{2,0,1:T(2,128)S(1)} all-gather(f32[2,16,128]{2,0,1:T(2,128)S(1)} %fusion.34), channel_id=1, replica_groups=mesh['mode'=4,'mesh'=8] {'mesh'}, dimensions={2}, use_global_device_ids=true | all-gather | bytes 147456 | tf_op jit(solution)/shard_map/all_gather | solution.py:63
  126.6 0.4 fusion.41
  127.0 0.4 fusion.33
  127.4 9.3 %all_gather.27 = f32[2,16,1024]{2,0,1:T(2,128)S(1)} all-gather(f32[2,16,128]{2,0,1:T(2,128)S(1)} %fusion.33), channel_id=1, replica_groups=mesh['mode'=4,'mesh'=8] {'mesh'}, dimensions={2}, use_global_device_ids=true | all-gather | bytes 147456 | tf_op jit(solution)/shard_map/all_gather | solution.py:63
  136.7 0.4 fusion.43
  137.1 0.3 convolution_select_fusion.3
  137.3 10.3 %all_gather.28 = bf16[2,16,1024]{2,0,1:T(2,128)(2,1)S(1)} all-gather(bf16[2,16,128]{2,0,1:T(2,128)(2,1)S(1)} %convert_bitcast_fusion.2), channel_id=1, replica_groups=mesh['mode'=4,'mesh'=8] {'mesh'}, dimensions={2}, use_global_device_ids=true | all-gather | bytes 73728 | tf_op jit(solution)/shard_map/all_gather | solution.py:67
  147.7 0.4 convolution_select_fusion.2
  148.1 9.0 %all_gather.29 = bf16[2,16,1024]{2,0,1:T(2,128)(2,1)S(1)} all-gather(bf16[2,16,128]{2,0,1:T(2,128)(2,1)S(1)} %convert_bitcast_fusion.1), channel_id=1, replica_groups=mesh['mode'=4,'mesh'=8] {'mesh'}, dimensions={2}, use_global_device_ids=true | all-gather | bytes 73728 | tf_op jit(solution)/shard_map/all_gather | solution.py:67
  157.1 0.4 convolution_select_fusion.1
  157.6 10.3 %all_gather.30 = bf16[2,16,1024]{2,0,1:T(2,128)(2,1)S(1)} all-gather(bf16[2,16,128]{2,0,1:T(2,128)(2,1)S(1)} %convert_bitcast_fusion), channel_id=1, replica_groups=mesh['mode'=4,'mesh'=8] {'mesh'}, dimensions={2}, use_global_device_ids=true | all-gather | bytes 73728 | tf_op jit(solution)/shard_map/all_gather | solution.py:67
  167.9 0.4 fusion.106
  168.3 0.6 copy.105
  169.0 9.0 %all_gather.31 = bf16[2,16,1024]{2,0,1:T(2,128)(2,1)S(1)} all-gather(bf16[2,16,128]{2,0,1:T(2,128)(2,1)S(1)} %get-tuple-element.37), channel_id=1, replica_groups=mesh['mode'=4,'mesh'=8] {'mesh'}, dimensions={2}, use_global_device_ids=true | all-gather | bytes 73728 | tf_op jit(solution)/shard_map/all_gather | solution.py:67
  177.9 9.3 %convolution_bitcast_fusion.2 = f32[2,16,20,128]{3,0,2,1:T(2,128)S(1)} fusion(bf16[16,20,128,128]{3,2,1,0:T(8,128)(2,1)} %param.10, bf16[128,16,2560]{2,0,1:T(8,128)(2,1)} %gather_fusion.1, pred[128]{0:T(512)(128)(4,1)S(1)} %get-tuple-element.32, bf16[2,16,2560]{2,0,1:T(2,128)(2,1)S(1)} %fusion.20, bf16[2,16,1024]{2,0,1:T(2,128)(2,1)S(1)} %all_gather.31, ...), kind=kOutput, calls=%fused_computation.21 | convolution fusion | flops 47431680 | bytes 21471748 | tf_op jit(solution)/shard_map/mkji,cmkj->cmki/dot_general | solution.py:186
  187.3 0.8 reshape.286
  (37 shorter events, 0.8 us)
Async XLA Ops:
  0.6 50.2 %copy-start = (bf16[16,128,128]{2,1,0:T(8,128)(2,1)S(1)}, bf16[16,128,128]{2,1,0:T(8,128)(2,1)}, u32[]{:S(2)}) copy-start(bf16[16,128,128]{2,1,0:T(8,128)(2,1)} %param.13) | copy-start | bytes 1572868
  0.6 24.8 %copy-start.4 = (s32[1,2,128]{2,1,0:T(2,128)S(1)}, s32[1,2,128]{2,1,0:T(2,128)}, u32[]{:S(2)}) copy-start(s32[1,2,128]{2,1,0:T(2,128)} %param.15) | copy-start | bytes 3076
  3.2 22.7 %collective-permute-start = (bf16[3,2,16,640]{3,2,1,0:T(8,128)(2,1)S(1)}, bf16[3,2,16,640]{3,2,1,0:T(8,128)(2,1)S(1)}, u32[]{:S(2)}, u32[]{:S(2)}) collective-permute-start(bf16[3,2,16,640]{3,2,1,0:T(8,128)(2,1)S(1)} %bitcast.217), channel_id=1, source_target_pairs={{0,8},{8,0},{16,24},{24,16},{1,9},{9,1},{17,25},{25,17},{2,10},{10... | collective-permute-start | bytes 368648 | tf_op jit(solution)/shard_map/ppermute | solution.py:30
  6.2 19.6 %collective-permute-start.1 = (bf16[3,2,16,640]{3,2,1,0:T(8,128)(2,1)S(1)}, bf16[3,2,16,640]{3,2,1,0:T(8,128)(2,1)S(1)}, u32[]{:S(2)}, u32[]{:S(2)}) collective-permute-start(bf16[3,2,16,640]{3,2,1,0:T(8,128)(2,1)S(1)} %bitcast.218), channel_id=1, source_target_pairs={{0,16},{8,24},{16,0},{24,8},{1,17},{9,25},{17,1},{25,9},{2,18},{10... | collective-permute-start | bytes 368648 | tf_op jit(solution)/shard_map/ppermute | solution.py:30
  7.8 18.0 %collective-permute-start.2 = (bf16[3,2,16,640]{3,2,1,0:T(8,128)(2,1)S(1)}, bf16[3,2,16,640]{3,2,1,0:T(8,128)(2,1)S(1)}, u32[]{:S(2)}, u32[]{:S(2)}) collective-permute-start(bf16[3,2,16,640]{3,2,1,0:T(8,128)(2,1)S(1)} %bitcast.220), channel_id=1, source_target_pairs={{0,24},{8,16},{16,8},{24,0},{1,25},{9,17},{17,9},{25,1},{2,26},{10... | collective-permute-start | bytes 368648 | tf_op jit(solution)/shard_map/ppermute | solution.py:30
  21.0 11.0 %all-to-all-start = ((bf16[4,2,30720]{2,1,0:T(2,128)(2,1)}), bf16[4,2,30720]{2,1,0:T(2,128)(2,1)S(1)}, u32[]{:S(2)}, u32[]{:S(2)}) async-start(bf16[4,2,30720]{2,1,0:T(2,128)(2,1)} %reshape.318), calls=%async_computation | async-start | bytes 983040 | tf_op jit(solution)/shard_map/all_to_all | solution.py:89
  47.2 31.1 %all-to-all-start.1 = ((bf16[3,2,64,640]{3,1,0,2:T(2,128)(2,1)}), bf16[3,2,64,640]{3,1,0,2:T(2,128)(2,1)S(1)}, u32[]{:S(2)}, u32[]{:S(2)}) async-start(bf16[3,2,64,640]{3,1,0,2:T(2,128)(2,1)} %copy.93), calls=%async_computation.1 | async-start | bytes 983040 | tf_op jit(solution)/shard_map/all_to_all | solution.py:98
  79.6 10.1 %copy-start.1 = (bf16[128,16,2560]{2,0,1:T(8,128)(2,1)S(1)}, bf16[128,16,2560]{2,0,1:T(8,128)(2,1)}, u32[]{:S(2)}) copy-start(bf16[128,16,2560]{2,0,1:T(8,128)(2,1)} %gather_fusion.1) | copy-start | bytes 31457284
  89.6 15.4 %copy-start.2 = (bf16[16,128,128]{2,1,0:T(8,128)(2,1)S(1)}, bf16[16,128,128]{2,1,0:T(8,128)(2,1)}, u32[]{:S(2)}) copy-start(bf16[16,128,128]{2,1,0:T(8,128)(2,1)} %param.12) | copy-start | bytes 1572868
  89.6 15.4 %copy-start.3 = (f32[2,16,128]{2,1,0:T(8,128)S(1)}, f32[2,16,128]{2,1,0:T(8,128)}, u32[]{:S(2)}) copy-start(f32[2,16,128]{2,1,0:T(8,128)} %param.14) | copy-start | bytes 49156
